TPU v7x, 32 devices: a whole 2x2x4 slice. The times are simulated.
32 devices in a mesh: batch: 4 (over z), seq: 8 (over y, x, core).
Axes of the slice: x: 2, y: 2, z: 4, core: 2. Of those that a mesh axis runs over, the one named last changes fastest.
Arguments:
- hidden: bfloat16 [4, 4096, 4096], P('batch', 'seq'), may hold values from -6 to 6
- score_direction: bfloat16 [4, 4096, 4096], P('batch', 'seq'), may hold values from -6 to 6
- adapter_down: bfloat16 [4096, 256], replicated, may hold values from -0.09375 to 0.09375
- adapter_up: bfloat16 [4096, 256], replicated, may hold values from -0.09375 to 0.09375
- rewards: float32 [4, 4096], P('batch', 'seq'), may hold values from -0.3125 to 0.3125
- values: float32 [4, 4096], P('batch', 'seq'), may hold values from -120 to 120
- log_ratio: float32 [4, 4096], P('batch', 'seq'), may hold values from -4 to 4
- lengths: int32 [4], P('batch'), may hold values from 1024 to 4096
Outputs:
- returns: float32 [4, 4096], P('batch', 'seq')
- grad_down: float32 [4096, 256], P(('batch', 'seq'))
- grad_up: float32 [4096, 256], P(('batch', 'seq'))
All inputs are finite; a program needn't handle non-finite values.
Results may differ from a plain program's by a relative error of at most 0.0029.
Values sent between devices are 32-bit elements; how exact they have to be, the bound alone decides.
No kernel may reach another device: no remote copies, remote signals or barrier semaphores. Data moves between devices by JAX's collectives and lax.ppermute only.
A program may use at most 128 MiB of HBM per device.

v0:
```python
import math
import jax
import jax.numpy as jnp
from jax import lax
from jax.sharding import PartitionSpec as P

ratio_cap = 2.0
weight_gain = 0.08


def local(hidden, score_direction, adapter_down, adapter_up, rewards, values, log_ratio, lengths):
    seq_count, shard_len, model_width = hidden.shape
    low_rank_product = adapter_down.shape[1]
    shard_total = lax.axis_size("seq")
    total_len = shard_len * shard_total
    seq_total = seq_count * lax.axis_size("batch")
    shard_id = lax.axis_index("seq")
    inner = jnp.arange(shard_len, dtype=jnp.int32)
    positions = shard_id * shard_len + inner
    valid = (positions[None, :] < lengths[:, None]).astype(jnp.float32)
    adapter_scale = 1.0 / math.sqrt(low_rank_product)
    down_projected = jnp.einsum(
        "ogz,zw->ogw", hidden, adapter_down, preferred_element_type=jnp.float32
    )
    up_projected = jnp.einsum(
        "ogz,zw->ogw", score_direction, adapter_up, preferred_element_type=jnp.float32
    )
    weight_update = adapter_scale * jnp.sum(down_projected * up_projected, axis=-1)
    importance = jnp.exp(log_ratio + weight_update)
    live = rewards * valid
    offsets = (inner[None, :] - inner[:, None]).astype(jnp.float32)
    discount_mat = jnp.where(offsets >= 0, jnp.exp(-offsets / total_len), jnp.zeros_like(offsets))
    within = jnp.einsum("sk,tk->st", live, discount_mat, precision=lax.Precision.HIGHEST)
    firsts = within[:, 0]
    every_first = lax.all_gather(firsts[:, None], "seq", axis=1, tiled=True)
    blocks = jnp.arange(shard_total, dtype=jnp.int32)
    steps_back = (blocks - shard_id - 1).astype(jnp.float32)
    weights_blk = jnp.where(
        blocks > shard_id, jnp.exp(-steps_back * shard_len / total_len), jnp.zeros_like(steps_back)
    )
    carried = jnp.sum(every_first * weights_blk[None, :], axis=1)
    tail_decay = jnp.exp(-(shard_len - inner).astype(jnp.float32) / total_len)
    returns = within + tail_decay[None, :] * carried[:, None]
    advantage = returns - values
    seq_weight = (
        weight_gain
        * math.sqrt(total_len * low_rank_product / seq_total)
        / lengths.astype(jnp.float32)
    )
    token_weights = valid * jnp.minimum(importance, ratio_cap) * advantage * seq_weight[:, None]
    up_scaled_map = (-adapter_scale * token_weights[:, :, None] * up_projected).astype(jnp.bfloat16)
    down_scaled_map = (-adapter_scale * token_weights[:, :, None] * down_projected).astype(
        jnp.bfloat16
    )
    group_total = lax.axis_size(("batch", "seq"))
    own_rows = model_width // group_total
    clip_norm = 0.5 * math.sqrt(2.0 * model_width * low_rank_product)
    partial_terms = jnp.concatenate(
        [
            jnp.einsum("oxe,oxq->eq", hidden, up_scaled_map, preferred_element_type=jnp.float32),
            jnp.einsum(
                "oxe,oxq->eq", score_direction, down_scaled_map, preferred_element_type=jnp.float32
            ),
        ],
        axis=1,
    )
    summed = lax.psum(partial_terms, ("batch", "seq"))
    squares = jnp.sum(summed * summed)
    own_part = lax.dynamic_slice_in_dim(
        summed, lax.axis_index(("batch", "seq")) * own_rows, own_rows, 0
    )
    grad_norm = jnp.sqrt(squares)
    factor = clip_norm / jnp.maximum(grad_norm, clip_norm)
    return (
        returns,
        own_part[:, :low_rank_product] * factor,
        own_part[:, low_rank_product:] * factor,
    )


def solution(mesh):
    placed = (
        P("batch", "seq", None),
        P("batch", "seq", None),
        P(),
        P(),
        P("batch", "seq"),
        P("batch", "seq"),
        P("batch", "seq"),
        P("batch"),
    )
    return jax.shard_map(
        local,
        mesh=mesh,
        in_specs=placed,
        out_specs=(P("batch", "seq"), P(("batch", "seq"), None), P(("batch", "seq"), None)),
        check_vma=False,
    )
```

profile of v0, /device:TPU:0, one launch (start us, length us, event | category | flops | bytes accessed | tf_op | source)
XLA Modules:
  0.0 237.2 jit_solution(16906972712396040121)
XLA Ops:
  7.2 0.0 copy-start
  7.2 0.0 all-reduce.3.cloned.1.call-start
  8.0 1.8 fusion.6
  9.9 0.5 slice.12
  10.4 1.2 dynamic-slice
  11.6 1.3 bitcast_dynamic-update-slice_fusion
  13.0 15.2 %all-reduce = f32[8]{0:T(128)S(1)} all-reduce(f32[8]{0:T(128)S(1)} %bitcast_dynamic-update-slice_fusion), channel_id=1, replica_groups=mesh['batch'=4,'seq'=8] {'seq'}, use_global_device_ids=true, to_apply=%add | all-reduce | flops 8 | bytes 64
  28.1 0.6 fusion.26
  28.7 0.0 copy-start.1
  28.7 4.3 %fusion.1 = f32[512,256]{0,1:T(8,128)S(1)} fusion(bf16[4096,256]{1,0:T(8,128)(2,1)} %param.11, bf16[1,512,4096]{2,1,0:T(8,128)(2,1)} %param.9), kind=kOutput, calls=%fused_computation.5 | convolution fusion | flops 1073741824 | bytes 6815744 | tf_op jit(solution)/shard_map/ogz,zw->ogw/dot_general | solution.py:25
  33.0 0.0 copy-done
  33.0 0.0 copy-done.1
  33.1 0.0 copy-start.4
  33.1 0.0 copy-start.5
  33.1 1.3 multiply_reduce_fusion.1
  34.5 0.7 multiply_add_fusion
  35.1 0.0 copy-start.3
  35.1 0.0 copy-done.4
  35.2 0.0 copy-done.5
  35.2 0.0 copy-start.2
  35.2 1.3 convolution_bitcast_fusion.1
  36.5 0.0 copy-done.3
  36.5 0.9 copy-done.2
  37.4 1.3 convolution_bitcast_fusion
  38.7 3.8 %pad_maximum_fusion = f32[4096,512]{0,1:T(8,128)} fusion(f32[4096,256]{0,1:T(8,128)S(1)} %convolution_bitcast_fusion, f32[4096,256]{0,1:T(8,128)S(1)} %convolution_bitcast_fusion.1), kind=kLoop, calls=%fused_computation | loop fusion | flops 2097152 | bytes 16777216 | tf_op jit(solution)/shard_map/concatenate | solution.py:58
  42.4 0.0 all-reduce.3.cloned.1.call-update
  42.4 178.5 %all-reduce.3.cloned.1.call-done = f32[4096,512]{0,1:T(8,128)} async-done(((f32[4096,512]{0,1:T(8,128)}), f32[4096,512]{0,1:T(8,128)}) %all-reduce.3.cloned.1.call-update) | async-done | bytes 8388624 | tf_op jit(solution)/shard_map/psum | solution.py:67
  220.9 6.1 %multiply_reduce_fusion = f32[]{:T(128)} fusion(f32[4096,512]{0,1:T(8,128)} %all-reduce.3.cloned.1.call-done), kind=kLoop, calls=%fused_computation.1 | loop fusion | flops 4194303 | bytes 8388612 | tf_op jit(solution)/shard_map/reduce_sum | solution.py:68
  227.8 1.0 dynamic-slice_multiply_fusion
  228.8 0.8 copy.12
  229.6 0.8 copy.11
  (3 shorter events, 0.0 us)
Async XLA Ops:
  7.2 25.9 %copy-start = (bf16[4096,256]{1,0:T(8,128)(2,1)S(1)}, bf16[4096,256]{1,0:T(8,128)(2,1)}, u32[]{:S(2)}) copy-start(bf16[4096,256]{1,0:T(8,128)(2,1)} %param.10) | copy-start | bytes 6291460
  7.2 213.7 %all-reduce.3.cloned.1.call-start = ((), (), s32[]{:S(2)}) async-start(), calls=%async_computation | async-start | bytes 16777216 | tf_op jit(solution)/shard_map/psum | solution.py:67
  28.7 4.3 %copy-start.1 = (bf16[1,512,4096]{2,1,0:T(8,128)(2,1)S(1)}, bf16[1,512,4096]{2,1,0:T(8,128)(2,1)}, u32[]{:S(2)}) copy-start(bf16[1,512,4096]{2,1,0:T(8,128)(2,1)} %param.8) | copy-start | bytes 12582916
  33.1 2.1 copy-start.4
  33.1 2.1 copy-start.5
  35.1 1.4 copy-start.3
  35.2 2.2 copy-start.2
Sparse Core Ops, SparseCore 0:
  42.6 178.3 all-reduce.2
where the time goes:
time: 237 us
  waiting for transfers between devices  178 us (75%)
  between operations  15.7 us (7%)
  blocking collectives  15.2 us (6%)
  other arithmetic  12.2 us (5%)
  matrix products  10 us (4%)
  local copies, waits for them, and re-layouts  5.52 us (2%)
    psum x1, waiting for transfers between devices, local(): summed = lax.psum(partial_terms, ('batch', 'seq'))  178 us
    unnamed x1, blocking collectives  15.2 us
    reduce_sum x1, other arithmetic, local(): squares = jnp.sum(summed * summed)  6.14 us
    unnamed x17, local copies, waits for them, and re-layouts  5 us
  transfers between devices with their start and end apart: 1, of which 1 were waited for; matrix products, arithmetic and copies ran while one was open for 0% of the time, Pallas kernels for 0%

commit v1 on v0

--- a/solution.py
+++ b/solution.py
@@ -64,7 +64,8 @@
         ],
         axis=1,
     )
-    summed = lax.psum(partial_terms, ("batch", "seq"))
+    half = lax.psum(partial_terms, "seq")
+    summed = lax.psum(half, "batch")
     squares = jnp.sum(summed * summed)
     own_part = lax.dynamic_slice_in_dim(
         summed, lax.axis_index(("batch", "seq")) * own_rows, own_rows, 0

time: 237 us -> 478 us (2.02)
  waiting for transfers between devices: 178 us -> 419 us
    psum x1 -> x2, waiting for transfers between devices: 178 us -> 419 us  [the longest x1 293 us: local(): summed = lax.psum(half, 'batch')]
  transfers between devices with their start and end apart: 1 -> 2, of which waited for: 1 -> 2; matrix products, arithmetic and copies ran while one was open for 0% -> 0% of each run, Pallas kernels for 0% -> 0%
where the time goes in v1:
time: 478 us
  waiting for transfers between devices  419 us (88%)
  between operations  15.8 us (3%)
  blocking collectives  15.2 us (3%)
  other arithmetic  12.2 us (3%)
  matrix products  10 us (2%)
  local copies, waits for them, and re-layouts  5.52 us (1%)
    psum x1, waiting for transfers between devices, local(): summed = lax.psum(half, 'batch')  293 us
    psum x1, waiting for transfers between devices, local(): half = lax.psum(partial_terms, 'seq')  126 us
    unnamed x1, blocking collectives  15.2 us
  transfers between devices with their start and end apart: 2, of which 2 were waited for; matrix products, arithmetic and copies ran while one was open for 0% of the time, Pallas kernels for 0%

profile of v1, /device:TPU:0, one launch (start us, length us, event | category | flops | bytes accessed | tf_op | source)
XLA Modules:
  0.0 477.9 jit_solution(5141042555328557608)
XLA Ops:
  7.2 0.0 copy-start
  7.2 0.0 all-reduce.4.cloned.1.call-start
  8.0 1.8 fusion.6
  9.9 0.5 slice.12
  10.4 1.2 dynamic-slice
  11.6 1.3 bitcast_dynamic-update-slice_fusion
  13.0 15.2 %all-reduce = f32[8]{0:T(128)S(1)} all-reduce(f32[8]{0:T(128)S(1)} %bitcast_dynamic-update-slice_fusion), channel_id=1, replica_groups=mesh['batch'=4,'seq'=8] {'seq'}, use_global_device_ids=true, to_apply=%add | all-reduce | flops 8 | bytes 64
  28.1 0.6 fusion.26
  28.7 4.3 fusion.1
  33.0 0.0 copy-done
  33.0 0.0 copy-done.1
  33.1 0.0 copy-start.4
  33.1 0.0 copy-start.5
  33.1 1.3 multiply_reduce_fusion.1
  34.5 0.7 multiply_add_fusion
  35.1 0.0 copy-start.3
  35.1 0.0 copy-done.4
  35.2 0.0 copy-done.5
  35.2 0.0 copy-start.2
  35.2 1.3 convolution_bitcast_fusion.1
  36.5 0.9 copy-done.2
  37.4 1.3 convolution_bitcast_fusion
  38.7 3.8 pad_maximum_fusion
  42.4 0.0 all-reduce.4.cloned.1.call-update
  42.4 0.0 all-reduce.6.cloned.1.call-start
  42.5 125.7 %all-reduce.4.cloned.1.call-done = f32[4096,512]{0,1:T(8,128)} async-done(((f32[4096,512]{0,1:T(8,128)}), f32[4096,512]{0,1:T(8,128)}) %all-reduce.4.cloned.1.call-update) | async-done | bytes 8388624 | tf_op jit(solution)/shard_map/psum | solution.py:67
  168.1 0.0 all-reduce.6.cloned.1.call-update
  168.2 293.4 %all-reduce.6.cloned.1.call-done = f32[4096,512]{0,1:T(8,128)} async-done(((f32[4096,512]{0,1:T(8,128)}), f32[4096,512]{0,1:T(8,128)}) %all-reduce.6.cloned.1.call-update) | async-done | bytes 8388624 | tf_op jit(solution)/shard_map/psum | solution.py:68
  461.6 6.1 %multiply_reduce_fusion = f32[]{:T(128)} fusion(f32[4096,512]{0,1:T(8,128)} %all-reduce.6.cloned.1.call-done), kind=kLoop, calls=%fused_computation.1 | loop fusion | flops 4194303 | bytes 8388612 | tf_op jit(solution)/shard_map/reduce_sum | solution.py:69
  468.5 1.0 dynamic-slice_multiply_fusion
  469.5 0.8 copy.12
  470.3 0.8 copy.11
  (5 shorter events, 0.0 us)
Async XLA Ops:
  7.2 25.9 %copy-start = (bf16[4096,256]{1,0:T(8,128)(2,1)S(1)}, bf16[4096,256]{1,0:T(8,128)(2,1)}, u32[]{:S(2)}) copy-start(bf16[4096,256]{1,0:T(8,128)(2,1)} %param.10) | copy-start | bytes 6291460
  7.2 161.0 %all-reduce.4.cloned.1.call-start = ((), (), s32[]{:S(2)}) async-start(), calls=%async_computation | async-start | bytes 16777216 | tf_op jit(solution)/shard_map/psum | solution.py:67
  28.7 4.3 copy-start.1
  33.1 2.1 copy-start.4
  33.1 2.1 copy-start.5
  35.1 1.4 copy-start.3
  35.2 2.2 copy-start.2
  42.4 419.2 %all-reduce.6.cloned.1.call-start = ((), (), s32[]{:S(2)}) async-start(), calls=%async_computation.1 | async-start | bytes 16777216 | tf_op jit(solution)/shard_map/psum | solution.py:68
Sparse Core Ops, SparseCore 0:
  42.6 125.5 all-reduce.3
  170.6 290.9 all-reduce.5
